TPU v7x, 32 devices: a whole 2x2x4 slice. The times are simulated.
32 devices in a mesh: seq: 8 (over y, x, core), exp: 4 (over z).
Axes of the slice: x: 2, y: 2, z: 4, core: 2. Of those that a mesh axis runs over, the one named last changes fastest.
Arguments:
- queries: bfloat16 [2048, 4096], P('seq', 'exp'), may hold values from -6 to 6
- key_rows: bfloat16 [2048, 512], P('seq'), may hold values from -6 to 6
- value_rows: bfloat16 [2048, 512], P('seq'), may hold values from -6 to 6
- sink_logits: float32 [64], P('exp'), may hold values from -2 to 2
- residual: bfloat16 [2048, 2880], P('seq'), may hold values from -6 to 6
- out_weight: bfloat16 [4096, 2880], P('exp'), may hold values from -0.375 to 0.375
- norm_gain: float32 [2880], replicated, may hold values from 0.25 to 1.75
- expert_ids: int32 [2048, 4], P('seq'), may hold values from 0 to 31, all different within a row; in each aligned block of 256 rows (0 to 255, 256 to 511, ...) at most 48 rows name the same one
- route_gates: float32 [2048, 4], P('seq'), may hold values from 0.1 to 0.6
- gate_proj: bfloat16 [32, 2880, 2048], P('seq', None, 'exp'), may hold values from -0.109375 to 0.109375
- up_proj: bfloat16 [32, 2880, 2048], P('seq', None, 'exp'), may hold values from -0.109375 to 0.109375
- down_proj: bfloat16 [32, 2048, 2880], P('seq', 'exp'), may hold values from -0.125 to 0.125
Outputs:
- layer_out: bfloat16 [2048, 2880], P('seq')
Inputs may be any that keep to these rules, and one draw needn't show every extreme that they name: `expert_ids`: each token names 4 different experts. In each slab of 256 tokens no expert is named by more than 48 entries, and that bound is reached.
All inputs are finite; a program needn't handle non-finite values.
Results may differ from a plain program's by a relative error of at most 0.018.
Values may be sent and summed in bfloat16 or wider, within the bound.
No kernel may reach another device: no remote copies, remote signals or barrier semaphores. Data moves between devices by JAX's collectives and lax.ppermute only.
A program may use at most 128 MiB of HBM per device.

v0:
```python
import math
import jax
import jax.numpy as jnp
from jax import lax
from jax.sharding import PartitionSpec as P

HQ = 64
HK = 8
HEAD = 64
TOP = 4
WIN = 128


def passed_along(x, axis, by):
    count = lax.axis_size(axis)
    pairs = [(i, i + by) for i in range(count) if 0 <= i + by < count]
    return lax.ppermute(x, axis, pairs)


def normalize(mixed, gain):
    wide_vals = mixed.astype(jnp.float32)
    inv_scale = lax.rsqrt(jnp.mean(wide_vals * wide_vals, axis=-1, keepdims=True) + 1e-05)
    return (wide_vals * inv_scale * gain).astype(jnp.bfloat16)


def activate(gate_acc, up_acc):
    gate_acc = jnp.minimum(gate_acc, 7.0)
    up_acc = jnp.clip(up_acc, -7.0, 7.0)
    return ((up_acc + 1.0) * gate_acc * jax.nn.sigmoid(1.702 * gate_acc)).astype(jnp.bfloat16)


def send_back(partial_out):
    return lax.all_to_all(partial_out, "seq", split_axis=0, concat_axis=0, tiled=True)


def on_device(
    queries,
    key_rows,
    value_rows,
    sink_logits,
    residual,
    out_weight,
    norm_gain,
    expert_ids,
    route_gates,
    gate_proj,
    up_proj,
    down_proj,
):
    tok_rows = queries.shape[0]
    local_heads = queries.shape[1] // HEAD
    per_group = HQ // HK
    column = lax.axis_index("exp")
    slab_index = lax.axis_index("seq")
    tail_rows = passed_along((key_rows[tok_rows - WIN :], value_rows[tok_rows - WIN :]), "seq", 1)
    key_full = jnp.concatenate([tail_rows[0], key_rows], 0)
    value_full = jnp.concatenate([tail_rows[1], value_rows], 0)
    kv_count = max(1, local_heads // per_group)
    kv_start = column * local_heads // per_group
    key_sel = lax.dynamic_slice_in_dim(key_full, kv_start * HEAD, kv_count * HEAD, 1).reshape(
        WIN + tok_rows, kv_count, HEAD
    )
    value_sel = lax.dynamic_slice_in_dim(value_full, kv_start * HEAD, kv_count * HEAD, 1).reshape(
        WIN + tok_rows, kv_count, HEAD
    )
    key_heads = jnp.repeat(key_sel, local_heads // kv_count, axis=1)
    value_heads = jnp.repeat(value_sel, local_heads // kv_count, axis=1)
    query_heads = queries.reshape(tok_rows, local_heads, HEAD)
    scores = jnp.einsum(
        "qhd,khd->hqk", query_heads, key_heads, preferred_element_type=jnp.float32
    ) * (1.0 / math.sqrt(HEAD))
    first_pos = slab_index * tok_rows
    q_pos = first_pos + jnp.arange(tok_rows, dtype=jnp.int32)
    k_pos = first_pos - WIN + jnp.arange(WIN + tok_rows, dtype=jnp.int32)
    allowed = (
        (k_pos[None, :] <= q_pos[:, None])
        & (k_pos[None, :] > q_pos[:, None] - WIN)
        & (k_pos[None, :] >= 0)
    )
    scores = jnp.where(allowed[None], scores, -1e30)
    row_top = jnp.maximum(jnp.max(scores, axis=-1), sink_logits[:, None])
    expo = jnp.exp(scores - row_top[..., None])
    denominator = jnp.sum(expo, axis=-1) + jnp.exp(sink_logits[:, None] - row_top)
    weights = (expo / denominator[..., None]).astype(jnp.bfloat16)
    context = jnp.einsum("hqk,khd->qhd", weights, value_heads, preferred_element_type=jnp.float32)
    context = context.astype(jnp.bfloat16).reshape(tok_rows, local_heads * HEAD)
    attn_part = jnp.dot(context, out_weight, preferred_element_type=jnp.float32)
    attn_out = lax.psum(attn_part.astype(jnp.bfloat16), "exp").astype(jnp.float32)
    mixed = (residual.astype(jnp.float32) + attn_out).astype(jnp.bfloat16)
    normed = normalize(mixed, norm_gain)
    local_experts = gate_proj.shape[0]
    seq_count = lax.axis_size("seq")
    experts = local_experts * seq_count
    cap = 3 * tok_rows * TOP // (2 * experts)
    flat_ids = expert_ids.reshape(-1)
    onehot = (flat_ids[:, None] == jnp.arange(experts, dtype=jnp.int32)[None, :]).astype(jnp.int32)
    rank_ids = jnp.cumsum(onehot, axis=0) - 1
    slot_ids = jnp.sum(rank_ids * onehot, axis=1)
    targets = flat_ids * cap + slot_ids
    source = (
        jnp.full((experts * cap,), -1, jnp.int32)
        .at[targets]
        .set(jnp.arange(tok_rows * TOP, dtype=jnp.int32))
    )
    filled = source >= 0
    token_of = jnp.where(filled, source // TOP, 0)
    packed = jnp.where(filled[:, None], normed[token_of], jnp.zeros((), jnp.bfloat16))
    packed = packed.reshape(seq_count, local_experts, cap, packed.shape[1])
    slot_block = lax.all_to_all(packed, "seq", split_axis=0, concat_axis=0, tiled=True)
    gate_acc = jnp.einsum(
        "secd,edf->secf", slot_block, gate_proj, preferred_element_type=jnp.float32
    )
    up_acc = jnp.einsum("secd,edf->secf", slot_block, up_proj, preferred_element_type=jnp.float32)
    hidden = activate(gate_acc, up_acc)
    partial_out = jnp.einsum(
        "secf,efd->secd", hidden, down_proj, preferred_element_type=jnp.float32
    ).astype(jnp.bfloat16)
    returned = send_back(partial_out)
    flat_back = returned.reshape(experts * cap, returned.shape[3])
    picked = flat_back[targets].astype(jnp.float32).reshape(tok_rows, TOP, returned.shape[3])
    moe_part = jnp.sum(picked * route_gates[:, :, None], axis=1)
    moe_total = lax.psum(moe_part.astype(jnp.bfloat16), "exp").astype(jnp.float32)
    return (mixed.astype(jnp.float32) + moe_total).astype(jnp.bfloat16)


def solution(mesh):
    return jax.shard_map(
        on_device,
        mesh=mesh,
        in_specs=(
            P("seq", "exp"),
            P("seq", None),
            P("seq", None),
            P("exp"),
            P("seq", None),
            P("exp", None),
            P(),
            P("seq", None),
            P("seq", None),
            P("seq", None, "exp"),
            P("seq", None, "exp"),
            P("seq", "exp", None),
        ),
        out_specs=P("seq", None),
        check_vma=False,
    )
```

profile of v0, /device:TPU:0, one launch (start us, length us, event | category | flops | bytes accessed | tf_op | source)
XLA Modules:
  0.0 490.9 jit_solution(17000879726990908606)
XLA Ops:
  6.5 1.1 copy.33
  7.7 2.4 collective-permute-start
  10.1 1.1 copy.35
  11.2 4.5 collective-permute-start.1
  15.8 1.2 copy.37
  17.0 0.8 copy.40
  18.3 1.2 fusion.11
  19.6 1.3 fusion.10
  21.1 1.8 fusion.34
  22.9 0.8 slice-done.1
  23.7 2.9 convolution_convert_fusion
  26.7 9.0 %reduce-window.6 = s32[32,8,128]{2,1,0:T(8,128)S(1)} reduce-window(s32[32,8,128]{2,1,0:T(8,128)S(1)} %fusion.37, s32[]{:T(128)} %constant.27.clone.1), window={size=1x1x128 pad=0_0x0_0x127_0}, to_apply=%region_3.4 | reduce-window | flops 4161536 | bytes 262148 | tf_op jit(solution)/shard_map/reduce-window
  36.5 4.5 scatter_custom_fusion
  41.2 52.9 %all-reduce.3.cloned.1.call-done = bf16[256,2880]{0,1:T(8,128)(2,1)} async-done(((bf16[256,2880]{0,1:T(8,128)(2,1)}), bf16[256,2880]{0,1:T(8,128)(2,1)}) %all-reduce.3.cloned.1.call-update) | async-done | bytes 1474576 | tf_op jit(solution)/shard_map/psum | solution.py:88
  94.1 1.9 fusion.13
  96.0 3.0 fusion.15
  99.1 1.8 copy.44
  100.9 8.1 %gather_fusion = bf16[1536,2880]{1,0:T(8,128)(2,1)} fusion(bf16[256,2880]{1,0:T(8,128)(2,1)S(1)} %copy.44, s32[2048]{0:T(1024)S(1)} %pad_clamp_fusion), kind=kCustom, calls=%fused_computation | custom fusion | bytes 17700864 | tf_op jit(solution)/shard_map/gather | solution.py:107
  109.0 8.0 %broadcast_select_fusion = bf16[8,4,48,2880]{3,2,1,0:T(8,128)(2,1)} fusion(bf16[8,4,48,2880]{3,2,1,0:T(8,128)(2,1)} %bitcast.70, pred[8,4,48]{2,1,0:T(4,128)(4,1)S(1)} %broadcast_in_dim.62), kind=kLoop, calls=%fused_computation.11 | loop fusion | flops 4423680 | bytes 17696256 | tf_op jit(solution)/shard_map/jit(_where)/select_n | solution.py:107
  117.0 104.8 %all_to_all.10 = bf16[8,4,48,2880]{3,2,1,0:T(8,128)(2,1)S(1)} all-to-all(bf16[8,4,48,2880]{3,2,1,0:T(8,128)(2,1)} %broadcast_select_fusion), channel_id=1, replica_groups=mesh['seq'=8,'exp'=4] {'seq'}, dimensions={0} | all-to-all | bytes 17694720 | tf_op jit(solution)/shard_map/all_to_all | solution.py:109
  221.8 3.5 copy-done.2
  225.3 9.6 %fusion.2 = f32[4,8,48,512]{3,2,1,0:T(8,128)} fusion(bf16[4,2880,512]{2,1,0:T(8,128)(2,1)} %param.21, bf16[8,4,48,2880]{3,2,1,0:T(8,128)(2,1)S(1)} %all_to_all.10), kind=kOutput, calls=%fused_computation.6 | convolution fusion | flops 4529848320 | bytes 23789568 | tf_op jit(solution)/shard_map/secd,edf->secf/dot_general | solution.py:110
  235.0 25.9 %convert_bitcast_fusion = bf16[8,4,48,2880]{3,2,0,1:T(8,128)(2,1)} fusion(bf16[4,512,2880]{1,2,0:T(8,128)(2,1)} %param.23, f32[4,8,48,512]{3,2,1,0:T(8,128)} %fusion.2, bf16[4,2880,512]{2,1,0:T(8,128)(2,1)} %param.22, bf16[8,4,48,2880]{3,2,1,0:T(8,128)(2,1)} %copy-done.2), kind=kOutput, calls=%fused_computation.10 | convolution fusion | flops 9071984640 | bytes 44433408 | tf_op jit(solution)/shard_map/secf,efd->secd/dot_general | solution.py:115
  260.8 7.9 %copy.47 = bf16[8,4,48,2880]{3,2,1,0:T(8,128)(2,1)} copy(bf16[8,4,48,2880]{3,2,0,1:T(8,128)(2,1)} %convert_bitcast_fusion) | data formatting | bytes 17694720 | tf_op jit(solution)/shard_map/convert_element_type | solution.py:117
  268.7 5.1 %all-to-all-start.1 = ((bf16[8,4,48,2880]{3,2,1,0:T(8,128)(2,1)}), bf16[8,4,48,2880]{3,2,1,0:T(8,128)(2,1)}, u32[]{:S(2)}, u32[]{:S(2)}) async-start(bf16[8,4,48,2880]{3,2,1,0:T(8,128)(2,1)} %copy.47), calls=%async_computation.1 | async-start | bytes 18087936 | tf_op jit(solution)/shard_map/all_to_all | solution.py:33
  274.3 100.6 %all-to-all-done.1 = bf16[8,4,48,2880]{3,2,1,0:T(8,128)(2,1)} async-done(((bf16[8,4,48,2880]{3,2,1,0:T(8,128)(2,1)}), bf16[8,4,48,2880]{3,2,1,0:T(8,128)(2,1)}, u32[]{:S(2)}, u32[]{:S(2)}) %all-to-all-start.1) | async-done | bytes 8847392 | tf_op jit(solution)/shard_map/all_to_all | solution.py:33
  374.9 16.4 %gather_fusion.1 = bf16[1024,2880]{1,0:T(8,128)(2,1)} fusion(bf16[1536,2880]{1,0:T(8,128)(2,1)} %bitcast.21, s32[1024]{0:T(1024)S(1)} %broadcast_clamp_fusion), kind=kCustom, calls=%fused_computation.1 | custom fusion | bytes 11800576 | tf_op jit(solution)/shard_map/gather | solution.py:120
  391.3 11.7 %reshape.236 = f32[256,4,2880]{2,1,0:T(4,128)} reshape(bf16[1024,2880]{1,0:T(8,128)(2,1)} %gather_fusion.1) | data formatting | bytes 17694720 | tf_op jit(solution)/shard_map/convert_element_type | solution.py:120
  403.0 12.1 %multiply_reduce_fusion = bf16[256,2880]{1,0:T(8,128)(2,1)} fusion(f32[256,4,2880]{2,1,0:T(4,128)} %reshape.236, f32[256,4]{1,0:T(8,128)S(1)} %copy.48), kind=kLoop, calls=%fused_computation.3 | loop fusion | flops 5160960 | bytes 13275136 | tf_op jit(solution)/shard_map/reduce_sum | solution.py:121
  415.1 2.5 copy.49
  417.7 63.3 %all-reduce.5.cloned.1.call-done = bf16[256,2880]{0,1:T(8,128)(2,1)} async-done(((bf16[256,2880]{0,1:T(8,128)(2,1)}), bf16[256,2880]{0,1:T(8,128)(2,1)}) %all-reduce.5.cloned.1.call-update) | async-done | bytes 1474576 | tf_op jit(solution)/shard_map/psum | solution.py:122
  481.0 3.0 fusion.16
  (56 shorter events, 2.2 us)
Async XLA Ops:
  6.5 87.5 %all-reduce.3.cloned.1.call-start = ((), (), s32[]{:S(2)}) async-start(), calls=%async_computation.2 | async-start | bytes 2949120 | tf_op jit(solution)/shard_map/psum | solution.py:88
  7.6 11.8 %copy-start.6 = (f32[16]{0:T(128)S(1)}, f32[16]{0:T(128)}, u32[]{:S(2)}) copy-start(f32[16]{0:T(128)} %param.15) | copy-start | bytes 196
  7.7 10.5 %collective-permute-start = (bf16[128,512]{0,1:T(8,128)(2,1)S(1)}, bf16[128,512]{0,1:T(8,128)(2,1)S(1)}, u32[]{:S(2)}, u32[]{:S(2)}) collective-permute-start(bf16[128,512]{0,1:T(8,128)(2,1)S(1)} %slice.20), channel_id=1, source_target_pairs={{0,4},{4,8},{8,12},{12,16},{16,20},{20,24},{24,28},{1,5},{5,9},{9,... | collective-permute-start | bytes 393224 | tf_op jit(solution)/shard_map/ppermute | solution.py:17
  11.2 7.0 %collective-permute-start.1 = (bf16[128,512]{0,1:T(8,128)(2,1)S(1)}, bf16[128,512]{0,1:T(8,128)(2,1)S(1)}, u32[]{:S(2)}, u32[]{:S(2)}) collective-permute-start(bf16[128,512]{0,1:T(8,128)(2,1)S(1)} %slice.21), channel_id=1, source_target_pairs={{0,4},{4,8},{8,12},{12,16},{16,20},{20,24},{24,28},{1,5},{5,9},{9,... | collective-permute-start | bytes 393224 | tf_op jit(solution)/shard_map/ppermute | solution.py:17
  20.9 2.0 slice-start
  21.0 2.6 slice-start.1
  23.7 12.4 %copy-start.3 = (s32[256,4]{0,1:T(4,128)S(1)}, s32[256,4]{0,1:T(4,128)}, u32[]{:S(2)}) copy-start(s32[256,4]{0,1:T(4,128)} %param.19) | copy-start | bytes 12292
  23.7 70.4 %copy-start = (bf16[256,2880]{0,1:T(8,128)(2,1)S(1)}, bf16[256,2880]{0,1:T(8,128)(2,1)}, u32[]{:S(2)}) copy-start(bf16[256,2880]{0,1:T(8,128)(2,1)} %param.16) | copy-start | bytes 4423684
  26.5 69.5 %copy-start.4 = (f32[2880]{0:T(1024)S(1)}, f32[2880]{0:T(1024)}, u32[]{:S(2)}) copy-start(f32[2880]{0:T(1024)} %param.18) | copy-start | bytes 34564
  221.8 3.5 copy-start.2
  268.7 5.4 %copy-start.5 = (f32[256,4]{0,1:T(4,128)S(1)}, f32[256,4]{0,1:T(4,128)}, u32[]{:S(2)}) copy-start(f32[256,4]{0,1:T(4,128)} %param.20) | copy-start | bytes 12292
  268.7 106.2 %all-to-all-start.1 = ((bf16[8,4,48,2880]{3,2,1,0:T(8,128)(2,1)}), bf16[8,4,48,2880]{3,2,1,0:T(8,128)(2,1)}, u32[]{:S(2)}, u32[]{:S(2)}) async-start(bf16[8,4,48,2880]{3,2,1,0:T(8,128)(2,1)} %copy.47), calls=%async_computation.1 | async-start | bytes 18087936 | tf_op jit(solution)/shard_map/all_to_all | solution.py:33
  273.8 207.2 %all-reduce.5.cloned.1.call-start = ((), (), s32[]{:S(2)}) async-start(), calls=%async_computation.3 | async-start | bytes 2949120 | tf_op jit(solution)/shard_map/psum | solution.py:122
  403.0 78.0 %copy-start.1 = (bf16[256,2880]{0,1:T(8,128)(2,1)S(1)}, bf16[256,2880]{0,1:T(8,128)(2,1)}, u32[]{:S(2)}) copy-start(bf16[256,2880]{0,1:T(8,128)(2,1)} %all-reduce.3.cloned.1.call-done) | copy-start | bytes 4423684
Sparse Core Ops, SparseCore 0:
  26.7 67.3 all-reduce.2
  417.8 63.1 all-reduce.4
where the time goes:
time: 492 us; the launch traced here: 491 us
  waiting for transfers between devices  217 us (44%)
  blocking collectives  105 us (21%)
  local copies, waits for them, and re-layouts  62.8 us (13%)
  matrix products  41.4 us (8%)
  other arithmetic  39 us (8%)
  between operations  13.8 us (3%)
  starting transfers between devices  12.3 us (2%)
    all_to_all x1, blocking collectives, on_device(): lax.all_to_all(packed, 'seq', split_axis=0, concat_axis=0, tiled=True)  105 us
    all_to_all x1, waiting for transfers between devices, send_back(): lax.all_to_all(partial_out, 'seq', split_axis=0, concat_axis=0, tiled=True)  101 us
    psum x1, waiting for transfers between devices, on_device(): lax.psum(moe_part.astype(jnp.bfloat16), 'exp').astype(jnp.float32)  63.3 us
    psum x1, waiting for transfers between devices, on_device(): lax.psum(attn_part.astype(jnp.bfloat16), 'exp').astype(jnp.float32)  52.9 us
    dot_general x1, matrix products, on_device(): jnp.einsum('secf,efd->secd', hidden, down_proj, preferred_element_type=jn...  25.9 us
    gather x1, local copies, waits for them, and re-layouts, on_device(): flat_back[targets].astype(jnp.float32)  16.4 us
    reduce_sum x1, other arithmetic, on_device(): moe_part = jnp.sum(picked * route_gates[:, :, None], axis=1)  12.1 us
    convert_element_type x1, local copies, waits for them, and re-layouts, on_device(): flat_back[targets].astype(jnp.float32)  11.7 us
  transfers between devices with their start and end apart: 5, of which 3 were waited for; matrix products, arithmetic and copies ran while one was open for 4% of the time, Pallas kernels for 0%

commit v1 on v0

--- a/solution.py
+++ b/solution.py
@@ -85,7 +85,9 @@
     context = jnp.einsum("hqk,khd->qhd", weights, value_heads, preferred_element_type=jnp.float32)
     context = context.astype(jnp.bfloat16).reshape(tok_rows, local_heads * HEAD)
     attn_part = jnp.dot(context, out_weight, preferred_element_type=jnp.float32)
-    attn_out = lax.psum(attn_part.astype(jnp.bfloat16), "exp").astype(jnp.float32)
+    attn_out = jnp.sum(lax.all_gather(attn_part.astype(jnp.bfloat16), "exp"), axis=0).astype(
+        jnp.float32
+    )
     mixed = (residual.astype(jnp.float32) + attn_out).astype(jnp.bfloat16)
     normed = normalize(mixed, norm_gain)
     local_experts = gate_proj.shape[0]

time: 492 us -> 559 us (1.14)
  waiting for transfers between devices: 217 us -> 261 us
  other arithmetic: 39 us -> 51.5 us
  local copies, waits for them, and re-layouts: 62.8 us -> 73.7 us
    all_gather x0 -> x1, waiting for transfers between devices: none -> 96.2 us  [on_device(): lax.all_gather(attn_part.astype(jnp.bfloat16), 'exp')]
    psum x1 -> x0, waiting for transfers between devices: 52.9 us -> none  [on_device(): lax.psum(attn_part.astype(jnp.bfloat16), 'exp').astype(jnp.float32)]
    reduce_sum x0 -> x1, other arithmetic: none -> 15.3 us  [on_device(): jnp.sum(lax.all_gather(attn_part.astype(jnp.bfloat16), 'exp'), axis=0)]
    all_gather x0 -> x1, local copies, waits for them, and re-layouts: none -> 11.6 us  [on_device(): lax.all_gather(attn_part.astype(jnp.bfloat16), 'exp')]
  transfers between devices with their start and end apart: 5 -> 5, of which waited for: 3 -> 3; matrix products, arithmetic and copies ran while one was open for 4% -> 3% of each run, Pallas kernels for 0% -> 0%
where the time goes in v1:
time: 559 us; the launch traced here: 558 us
  waiting for transfers between devices  261 us (47%)
  blocking collectives  105 us (19%)
  local copies, waits for them, and re-layouts  73.7 us (13%)
  other arithmetic  51.5 us (9%)
  matrix products  41.4 us (7%)
  between operations  13.8 us (2%)
  starting transfers between devices  12.3 us (2%)
    all_to_all x1, blocking collectives, on_device(): lax.all_to_all(packed, 'seq', split_axis=0, concat_axis=0, tiled=True)  105 us
    all_to_all x1, waiting for transfers between devices, send_back(): lax.all_to_all(partial_out, 'seq', split_axis=0, concat_axis=0, tiled=True)  101 us
    all_gather x1, waiting for transfers between devices, on_device(): lax.all_gather(attn_part.astype(jnp.bfloat16), 'exp')  96.2 us
    psum x1, waiting for transfers between devices, on_device(): lax.psum(moe_part.astype(jnp.bfloat16), 'exp').astype(jnp.float32)  63.8 us
    dot_general x1, matrix products, on_device(): jnp.einsum('secf,efd->secd', hidden, down_proj, preferred_element_type=jn...  25.9 us
    gather x1, local copies, waits for them, and re-layouts, on_device(): flat_back[targets].astype(jnp.float32)  16.4 us
    reduce_sum x1, other arithmetic, on_device(): jnp.sum(lax.all_gather(attn_part.astype(jnp.bfloat16), 'exp'), axis=0)  15.3 us
    reduce_sum x1, other arithmetic, on_device(): moe_part = jnp.sum(picked * route_gates[:, :, None], axis=1)  12.1 us
  transfers between devices with their start and end apart: 5, of which 3 were waited for; matrix products, arithmetic and copies ran while one was open for 3% of the time, Pallas kernels for 0%

profile of v1, /device:TPU:0, one launch (start us, length us, event | category | flops | bytes accessed | tf_op | source)
XLA Modules:
  0.0 558.1 jit_solution(9907871279645754166)
XLA Ops:
  6.5 1.1 copy.69
  7.7 2.4 collective-permute-start
  10.1 1.1 copy.71
  11.2 4.5 collective-permute-start.1
  15.8 1.2 copy.73
  17.4 1.2 fusion.11
  18.6 1.3 fusion.10
  20.1 1.8 fusion.34
  22.7 2.9 convolution_convert_fusion
  26.0 9.0 %reduce-window.6 = s32[32,8,128]{2,1,0:T(8,128)S(1)} reduce-window(s32[32,8,128]{2,1,0:T(8,128)S(1)} %fusion.37, s32[]{:T(128)} %constant.27.clone.1), window={size=1x1x128 pad=0_0x0_0x127_0}, to_apply=%region_3.4 | reduce-window | flops 4161536 | bytes 262148 | tf_op jit(solution)/shard_map/reduce-window
  35.9 4.5 scatter_custom_fusion
  40.5 96.2 %all-gather.3.cloned.1.call-done = bf16[1024,2880]{0,1:T(8,128)(2,1)} async-done(((bf16[256,2880]{0,1:T(8,128)(2,1)}), bf16[1024,2880]{0,1:T(8,128)(2,1)}) %all-gather.3.cloned.1.call-update) | async-done | bytes 5898256 | tf_op jit(solution)/shard_map/all_gather | solution.py:88
  136.7 11.6 %reshape.261 = bf16[4,256,2880]{1,0,2:T(4,128)(2,1)} reshape(bf16[1024,2880]{0,1:T(8,128)(2,1)} %all-gather.3.cloned.1.call-done) | data formatting | bytes 11796480 | tf_op jit(solution)/shard_map/all_gather | solution.py:88
  148.3 15.3 %reduce_sum.51 = bf16[256,2880]{0,1:T(8,128)(2,1)S(1)} reduce(bf16[4,256,2880]{1,0,2:T(4,128)(2,1)} %reshape.261, bf16[]{:T(256)} %constant.81.clone.1), dimensions={0}, to_apply=%region_2.3 | reduce | flops 2211840 | bytes 7372802 | tf_op jit(solution)/shard_map/reduce_sum | solution.py:88
  163.6 0.6 fusion.13
  164.2 1.7 fusion.15
  165.8 1.8 copy.80
  167.7 8.1 %gather_fusion = bf16[1536,2880]{1,0:T(8,128)(2,1)} fusion(bf16[256,2880]{1,0:T(8,128)(2,1)S(1)} %copy.80, s32[2048]{0:T(1024)S(1)} %pad_clamp_fusion), kind=kCustom, calls=%fused_computation | custom fusion | bytes 17700864 | tf_op jit(solution)/shard_map/gather | solution.py:109
  175.8 8.0 %broadcast_select_fusion = bf16[8,4,48,2880]{3,2,1,0:T(8,128)(2,1)} fusion(bf16[8,4,48,2880]{3,2,1,0:T(8,128)(2,1)} %bitcast.72, pred[8,4,48]{2,1,0:T(4,128)(4,1)S(1)} %broadcast_in_dim.62), kind=kLoop, calls=%fused_computation.11 | loop fusion | flops 4423680 | bytes 17696256 | tf_op jit(solution)/shard_map/jit(_where)/select_n | solution.py:109
  183.8 104.8 %all_to_all.10 = bf16[8,4,48,2880]{3,2,1,0:T(8,128)(2,1)S(1)} all-to-all(bf16[8,4,48,2880]{3,2,1,0:T(8,128)(2,1)} %broadcast_select_fusion), channel_id=1, replica_groups=mesh['seq'=8,'exp'=4] {'seq'}, dimensions={0} | all-to-all | bytes 17694720 | tf_op jit(solution)/shard_map/all_to_all | solution.py:111
  288.6 3.5 copy-done.2
  292.1 9.6 %fusion.2 = f32[4,8,48,512]{3,2,1,0:T(8,128)} fusion(bf16[4,2880,512]{2,1,0:T(8,128)(2,1)} %param.21, bf16[8,4,48,2880]{3,2,1,0:T(8,128)(2,1)S(1)} %all_to_all.10), kind=kOutput, calls=%fused_computation.6 | convolution fusion | flops 4529848320 | bytes 23789568 | tf_op jit(solution)/shard_map/secd,edf->secf/dot_general | solution.py:112
  301.8 25.9 %convert_bitcast_fusion = bf16[8,4,48,2880]{3,2,0,1:T(8,128)(2,1)} fusion(bf16[4,512,2880]{1,2,0:T(8,128)(2,1)} %param.23, f32[4,8,48,512]{3,2,1,0:T(8,128)} %fusion.2, bf16[4,2880,512]{2,1,0:T(8,128)(2,1)} %param.22, bf16[8,4,48,2880]{3,2,1,0:T(8,128)(2,1)} %copy-done.2), kind=kOutput, calls=%fused_computation.10 | convolution fusion | flops 9071984640 | bytes 44433408 | tf_op jit(solution)/shard_map/secf,efd->secd/dot_general | solution.py:117
  327.6 7.9 %copy.83 = bf16[8,4,48,2880]{3,2,1,0:T(8,128)(2,1)} copy(bf16[8,4,48,2880]{3,2,0,1:T(8,128)(2,1)} %convert_bitcast_fusion) | data formatting | bytes 17694720 | tf_op jit(solution)/shard_map/convert_element_type | solution.py:119
  335.5 5.3 all-to-all-start.1
  341.1 100.6 %all-to-all-done.1 = bf16[8,4,48,2880]{3,2,1,0:T(8,128)(2,1)} async-done(((bf16[8,4,48,2880]{3,2,1,0:T(8,128)(2,1)}), bf16[8,4,48,2880]{3,2,1,0:T(8,128)(2,1)}, u32[]{:S(2)}, u32[]{:S(2)}) %all-to-all-start.1) | async-done | bytes 8847392 | tf_op jit(solution)/shard_map/all_to_all | solution.py:33
  441.7 16.4 %gather_fusion.1 = bf16[1024,2880]{1,0:T(8,128)(2,1)} fusion(bf16[1536,2880]{1,0:T(8,128)(2,1)} %bitcast.21, s32[1024]{0:T(1024)S(1)} %broadcast_clamp_fusion), kind=kCustom, calls=%fused_computation.1 | custom fusion | bytes 11800576 | tf_op jit(solution)/shard_map/gather | solution.py:122
  458.1 11.7 %reshape.236 = f32[256,4,2880]{2,1,0:T(4,128)} reshape(bf16[1024,2880]{1,0:T(8,128)(2,1)} %gather_fusion.1) | data formatting | bytes 17694720 | tf_op jit(solution)/shard_map/convert_element_type | solution.py:122
  469.8 12.1 %multiply_reduce_fusion = bf16[256,2880]{1,0:T(8,128)(2,1)} fusion(f32[256,4,2880]{2,1,0:T(4,128)} %reshape.236, f32[256,4]{1,0:T(8,128)S(1)} %copy.84), kind=kLoop, calls=%fused_computation.3 | loop fusion | flops 5160960 | bytes 13275136 | tf_op jit(solution)/shard_map/reduce_sum | solution.py:123
  481.9 2.5 copy.85
  484.5 63.8 %all-reduce.2.cloned.1.call-done = bf16[256,2880]{0,1:T(8,128)(2,1)} async-done(((bf16[256,2880]{0,1:T(8,128)(2,1)}), bf16[256,2880]{0,1:T(8,128)(2,1)}) %all-reduce.2.cloned.1.call-update) | async-done | bytes 1474576 | tf_op jit(solution)/shard_map/psum | solution.py:124
  548.2 3.0 fusion.16
  (58 shorter events, 2.9 us)
Async XLA Ops:
  6.5 130.1 %all-gather.3.cloned.1.call-start = ((), (), s32[]{:S(2)}) async-start(), calls=%async_computation.3 | async-start | bytes 7372800 | tf_op jit(solution)/shard_map/all_gather | solution.py:88
  7.6 10.9 %copy-start.6 = (f32[16]{0:T(128)S(1)}, f32[16]{0:T(128)}, u32[]{:S(2)}) copy-start(f32[16]{0:T(128)} %param.15) | copy-start | bytes 196
  7.7 9.5 %collective-permute-start = (bf16[128,512]{0,1:T(8,128)(2,1)S(1)}, bf16[128,512]{0,1:T(8,128)(2,1)S(1)}, u32[]{:S(2)}, u32[]{:S(2)}) collective-permute-start(bf16[128,512]{0,1:T(8,128)(2,1)S(1)} %slice.20), channel_id=1, source_target_pairs={{0,4},{4,8},{8,12},{12,16},{16,20},{20,24},{24,28},{1,5},{5,9},{9,... | collective-permute-start | bytes 393224 | tf_op jit(solution)/shard_map/ppermute | solution.py:17
  11.2 6.0 %collective-permute-start.1 = (bf16[128,512]{0,1:T(8,128)(2,1)S(1)}, bf16[128,512]{0,1:T(8,128)(2,1)S(1)}, u32[]{:S(2)}, u32[]{:S(2)}) collective-permute-start(bf16[128,512]{0,1:T(8,128)(2,1)S(1)} %slice.21), channel_id=1, source_target_pairs={{0,4},{4,8},{8,12},{12,16},{16,20},{20,24},{24,28},{1,5},{5,9},{9,... | collective-permute-start | bytes 393224 | tf_op jit(solution)/shard_map/ppermute | solution.py:17
  20.0 2.2 slice-start
  20.1 2.6 slice-start.1
  22.7 2.9 copy-start.3
  148.3 15.3 %copy-start = (bf16[256,2880]{0,1:T(8,128)(2,1)S(1)}, bf16[256,2880]{0,1:T(8,128)(2,1)}, u32[]{:S(2)}) copy-start(bf16[256,2880]{0,1:T(8,128)(2,1)} %param.16) | copy-start | bytes 4423684
  148.3 15.9 %copy-start.4 = (f32[2880]{0:T(1024)S(1)}, f32[2880]{0:T(1024)}, u32[]{:S(2)}) copy-start(f32[2880]{0:T(1024)} %param.18) | copy-start | bytes 34564
  288.6 3.5 copy-start.2
  335.5 5.4 copy-start.5
  335.5 106.2 %all-to-all-start.1 = ((bf16[8,4,48,2880]{3,2,1,0:T(8,128)(2,1)}), bf16[8,4,48,2880]{3,2,1,0:T(8,128)(2,1)}, u32[]{:S(2)}, u32[]{:S(2)}) async-start(bf16[8,4,48,2880]{3,2,1,0:T(8,128)(2,1)} %copy.83), calls=%async_computation.1 | async-start | bytes 18087936 | tf_op jit(solution)/shard_map/all_to_all | solution.py:33
  340.9 207.4 %all-reduce.2.cloned.1.call-start = ((), (), s32[]{:S(2)}) async-start(), calls=%async_computation.2 | async-start | bytes 2949120 | tf_op jit(solution)/shard_map/psum | solution.py:124
  469.8 78.4 %copy-start.1 = (bf16[256,2880]{0,1:T(8,128)(2,1)S(1)}, bf16[256,2880]{0,1:T(8,128)(2,1)}, u32[]{:S(2)}) copy-start(bf16[256,2880]{0,1:T(8,128)(2,1)} %param.16) | copy-start | bytes 4423684
Sparse Core Ops, SparseCore 0:
  25.7 110.8 all-gather.2
  484.6 63.6 all-reduce.1
